TPU v7x, 32 devices: a whole 2x2x4 slice. The times are simulated.
32 devices in a mesh: gx: 4 (over y, x), gy: 2 (over core), gz: 4 (over z).
Axes of the slice: x: 2, y: 2, z: 4, core: 2. Of those that a mesh axis runs over, the one named last changes fastest.
Arguments:
- measures: float32 [65536, 256], P(('gx', 'gy', 'gz')), may hold values from -6 to 6
- group_index: int32 [65536], P(('gx', 'gy', 'gz')), may hold values from 0 to 511, as said below
- distinct_keys: int32 [32, 512], P(('gx', 'gy', 'gz')), may hold values from 32 to 65567, as said below
- group_counts: int32 [32], P(('gx', 'gy', 'gz')), may hold values from 128 to 512, as said below
Outputs:
- group_sums: float32 [16384, 256], P(('gx', 'gy', 'gz'))
- group_rows: int32 [16384], P(('gx', 'gy', 'gz'))
- group_keys: int32 [16384], P(('gx', 'gy', 'gz'))
- group_total: int32 [], replicated
Inputs may be any that keep to these rules, and one draw needn't show every extreme that they name: `group_counts`: every device has between 128 and 512 groups, and some device has exactly 512. `group_index`: each row's index lies below its device's group count, and every group of a device has at least one row. `distinct_keys`: each device's keys rise strictly; all keys of device d equal d modulo 32, so no key lives on two devices; entries at and past the device's count are unused.
All inputs are finite; a program needn't handle non-finite values.
Results may differ from a plain program's by a relative error of at most 0.0003.
Values sent between devices are 32-bit elements; how exact they have to be, the bound alone decides.
A program may use at most 64 MiB of HBM per device.

v0:
```python
import jax
import jax.numpy as jnp
from jax import lax
from jax.sharding import PartitionSpec as P


def shards(measures, group_index, distinct_keys, group_counts):
    rows, width = measures.shape
    span = distinct_keys.shape[1]
    devices = lax.axis_size(("gx", "gy", "gz"))
    slots = span // devices
    plane = lax.axis_size("gx") * lax.axis_size("gy")
    line = lax.axis_size("gz")
    count = group_counts[0]
    myself = jnp.int32(0)
    sender_counts = lax.all_gather(group_counts, ("gx", "gy", "gz"), axis=0, tiled=True)
    sender_offsets = jnp.cumsum(sender_counts) - sender_counts
    myself = lax.axis_index(("gx", "gy", "gz"))
    offset = sender_offsets[myself]
    group_total = jnp.sum(sender_counts)
    block = min(1024, rows)
    labels = lax.broadcasted_iota(jnp.int32, (span, block), 0)

    def accumulate(step, carry):
        totals, tallies = carry
        start = step * block
        index = lax.dynamic_slice_in_dim(group_index, start, block)
        values = lax.dynamic_slice_in_dim(measures, start, block, 0)
        hits = index[None, :] == labels
        totals = totals + jnp.dot(
            hits.astype(jnp.float32),
            values,
            precision=lax.Precision.HIGHEST,
            preferred_element_type=jnp.float32,
        )
        tallies = tallies + jnp.sum(hits, axis=1, dtype=jnp.int32)
        return (totals, tallies)

    sums, tallies = lax.fori_loop(
        0,
        rows // block,
        accumulate,
        (jnp.zeros((span, width), jnp.float32), jnp.zeros((span,), jnp.int32)),
    )
    local = jnp.arange(span, dtype=jnp.int32)
    live = local < count
    keys = jnp.where(live, distinct_keys[0], -1)
    fields = jnp.stack([tallies.astype(jnp.float32), keys.astype(jnp.float32)], axis=1)
    extra = fields.shape[1]

    def arrange(array):
        shaped = array.reshape((slots, devices) + array.shape[1:])
        rolled = jnp.roll(shaped, offset, axis=1)
        return rolled.reshape((slots, plane, line) + array.shape[1:])

    outgoing = (arrange(sums), arrange(fields))
    arrived = (
        lax.all_to_all(
            lax.all_to_all(outgoing[0], "gz", split_axis=2, concat_axis=2, tiled=True),
            ("gx", "gy"),
            split_axis=1,
            concat_axis=1,
            tiled=True,
        ),
        lax.all_to_all(
            lax.all_to_all(outgoing[1], "gz", split_axis=2, concat_axis=2, tiled=True),
            ("gx", "gy"),
            split_axis=1,
            concat_axis=1,
            tiled=True,
        ),
    )
    got_sums, got_fields = arrived
    got_fields = got_fields.reshape(-1, extra)
    sender = jnp.arange(devices, dtype=jnp.int32).reshape(1, plane, line)
    start_of = sender_offsets.reshape(1, plane, line)
    count_of = sender_counts.reshape(1, plane, line)
    level = jnp.arange(slots, dtype=jnp.int32).reshape(slots, 1, 1)
    position = level * devices + (myself - start_of) % devices
    arrived_live = (position < count_of) & (sender >= 0)
    target = jnp.where(arrived_live, (start_of + position) // devices, span).reshape(-1)
    group_sums = (
        jnp.zeros((span, width), jnp.float32)
        .at[target]
        .set(got_sums.reshape(-1, width), mode="drop")
    )
    group_rows = (
        jnp.zeros((span,), jnp.int32)
        .at[target]
        .set(got_fields[:, 0].astype(jnp.int32), mode="drop")
    )
    group_keys = (
        jnp.full((span,), -1, jnp.int32)
        .at[target]
        .set(got_fields[:, 1].astype(jnp.int32), mode="drop")
    )
    return (group_sums, group_rows, group_keys, group_total)


def solution(mesh):
    return jax.shard_map(
        shards,
        mesh=mesh,
        in_specs=(
            P(("gx", "gy", "gz"), None),
            P(("gx", "gy", "gz")),
            P(("gx", "gy", "gz"), None),
            P(("gx", "gy", "gz")),
        ),
        out_specs=(P(("gx", "gy", "gz"), None), P(("gx", "gy", "gz")), P(("gx", "gy", "gz")), P()),
        check_vma=False,
    )
```

profile of v0, /device:TPU:0, one launch (start us, length us, event | category | flops | bytes accessed | tf_op | source)
XLA Modules:
  0.0 106.3 jit_solution(15189355763401430567)
XLA Ops:
  1.4 42.0 %all-reduce = s32[32]{0:T(128)S(1)} all-reduce(s32[32]{0:T(128)S(1)} %dynamic-update-slice), channel_id=1, replica_groups=mesh['gx'=4,'gy'=2,'gz'=4] {'gx','gy','gz'}, use_global_device_ids=true, to_apply=%add | all-reduce | flops 32 | bytes 256
  43.6 0.6 fusion.19
  44.3 0.6 dynamic_slice.25
  46.8 7.4 %while.16 = (s32[]{:T(128)}, f32[512,256]{1,0:T(8,128)S(1)}, s32[512]{0:T(512)S(1)}, s32[2048]{0:T(1024)}, f32[2048,256]{1,0:T(8,128)}, /*index=5*/s32[]{:T(128)}, s32[]{:T(128)}, s32[]{:T(128)}, s32[]{:T(128)}) while((s32[]{:T(128)}, f32[512,256]{1,0:T(8,128)S(1)}, s32[512]{0:T(512)S(1)}, s32[2048]{0:T(1024)}, ...), condition=%wide.region_3.4_spmd.clone, body=%wide.region_1.3_spmd.clone.sunk | while | flops 1612972544 | bytes 2121886 | solution.py:39
  46.9 0.7 dynamic_slice.55
  47.6 2.7 %fusion.24 = f32[512,256]{1,0:T(8,128)S(1)} fusion(f32[2048,256]{1,0:T(8,128)} %get-tuple-element.203, s32[]{:T(128)S(6)} %select_n.107, s32[1024]{0:T(1024)S(1)} %dynamic_slice.55, f32[512,256]{1,0:T(8,128)S(1)} %get-tuple-element.191, pred[]{:T(512)S(6)} %compare.20), kind=kOutput, calls=%fused_computation.8.clone.1 | convolution fusion | flops 1611399168 | bytes 2101253 | tf_op jit(solution)/shard_map/while/body/eval_jaxpr/dot_general | solution.py:30
  50.2 0.3 fusion.25
  50.6 0.7 dynamic_slice.55
  51.2 2.7 %fusion.24 = f32[512,256]{1,0:T(8,128)S(1)} fusion(f32[2048,256]{1,0:T(8,128)} %get-tuple-element.203, s32[]{:T(128)S(6)} %select_n.107, s32[1024]{0:T(1024)S(1)} %dynamic_slice.55, f32[512,256]{1,0:T(8,128)S(1)} %get-tuple-element.191, pred[]{:T(512)S(6)} %compare.20), kind=kOutput, calls=%fused_computation.8.clone.1 | convolution fusion | flops 1611399168 | bytes 2101253 | tf_op jit(solution)/shard_map/while/body/eval_jaxpr/dot_general | solution.py:30
  53.9 0.3 fusion.25
  54.3 0.5 broadcast.199
  54.8 0.7 reduce.5
  55.8 0.7 reshape.312
  56.5 3.6 %all-to-all-start.2 = ((f32[4,1,256]{2,1,0:T(1,128)}), f32[4,1,256]{2,1,0:T(1,128)S(1)}, u32[]{:S(2)}, u32[]{:S(2)}) async-start(f32[4,1,256]{2,1,0:T(1,128)} %reshape.312), calls=%async_computation.2 | async-start | bytes 8192 | tf_op jit(solution)/shard_map/all_to_all | solution.py:66
  60.2 0.3 copy.38
  60.5 1.1 %copy.39 = f32[16,8,4,256]{3,1,0,2:T(8,128)} copy(f32[16,8,4,256]{3,0,2,1:T(8,128)S(1)} %bitcast.23) | data formatting | bytes 1048576 | tf_op jit(solution)/shard_map/reshape | solution.py:54
  61.6 4.0 %all-to-all-done.2 = f32[4,1,256]{2,1,0:T(1,128)S(1)} async-done(((f32[4,1,256]{2,1,0:T(1,128)}), f32[4,1,256]{2,1,0:T(1,128)S(1)}, u32[]{:S(2)}, u32[]{:S(2)}) %all-to-all-start.2) | async-done | bytes 4128 | tf_op jit(solution)/shard_map/all_to_all | solution.py:66
  65.6 3.5 %all-to-all-start = ((f32[16,8,4,256]{3,1,0,2:T(8,128)}), f32[16,8,4,256]{3,1,0,2:T(8,128)S(1)}, u32[]{:S(2)}, u32[]{:S(2)}) async-start(f32[16,8,4,256]{3,1,0,2:T(8,128)} %copy.39), calls=%async_computation | async-start | bytes 1048576 | tf_op jit(solution)/shard_map/all_to_all | solution.py:59
  69.3 0.5 broadcast.200
  69.8 0.7 reduce.6
  70.6 0.7 reshape.314
  71.3 10.3 %all-to-all-done = f32[16,8,4,256]{3,1,0,2:T(8,128)S(1)} async-done(((f32[16,8,4,256]{3,1,0,2:T(8,128)}), f32[16,8,4,256]{3,1,0,2:T(8,128)S(1)}, u32[]{:S(2)}, u32[]{:S(2)}) %all-to-all-start) | async-done | bytes 524320 | tf_op jit(solution)/shard_map/all_to_all | solution.py:59
  81.6 3.6 %all-to-all-start.3 = ((f32[8,1,128]{2,1,0:T(1,128)}), f32[8,1,128]{2,1,0:T(1,128)S(1)}, u32[]{:S(2)}, u32[]{:S(2)}) async-start(f32[8,1,128]{2,1,0:T(1,128)} %reshape.314), calls=%async_computation.3 | async-start | bytes 8192 | tf_op jit(solution)/shard_map/all_to_all | solution.py:65
  85.2 1.1 %copy.40 = f32[16,8,4,256]{3,2,0,1:T(4,128)} copy(f32[16,8,4,256]{3,1,0,2:T(8,128)S(1)} %all-to-all-done) | data formatting | bytes 1048576 | tf_op jit(solution)/shard_map/all_to_all | solution.py:59
  86.4 3.5 %all-to-all-done.3 = f32[8,1,128]{2,1,0:T(1,128)S(1)} async-done(((f32[8,1,128]{2,1,0:T(1,128)}), f32[8,1,128]{2,1,0:T(1,128)S(1)}, u32[]{:S(2)}, u32[]{:S(2)}) %all-to-all-start.3) | async-done | bytes 4128 | tf_op jit(solution)/shard_map/all_to_all | solution.py:65
  89.8 3.5 %all-to-all-start.1 = ((f32[16,8,4,256]{3,2,0,1:T(4,128)}), f32[16,8,4,256]{3,2,0,1:T(4,128)S(1)}, u32[]{:S(2)}, u32[]{:S(2)}) async-start(f32[16,8,4,256]{3,2,0,1:T(4,128)} %copy.40), calls=%async_computation.1 | async-start | bytes 1048576 | tf_op jit(solution)/shard_map/all_to_all | solution.py:58
  93.7 0.7 reduce.7
  94.8 3.0 %scatter_custom_fusion.1 = s32[512]{0:T(512)} fusion(s32[512]{0:T(512)S(1)} %bitcast.30, s32[512]{0:T(512)S(1)} %bitcast.34, s32[]{:T(128)} %constant.107.clone.1), kind=kCustom, calls=%fused_computation.40 | custom fusion | bytes 2052 | tf_op jit(solution)/shard_map/scatter | solution.py:90
  97.8 3.0 %scatter_custom_fusion.2 = s32[512]{0:T(512)} fusion(s32[512]{0:T(512)S(1)} %bitcast.31, s32[512]{0:T(512)S(1)} %bitcast.33, s32[]{:T(128)} %constant.111.clone.1), kind=kCustom, calls=%fused_computation.38 | custom fusion | bytes 2052 | tf_op jit(solution)/shard_map/scatter | solution.py:95
  100.8 2.2 %all-to-all-done.1 = f32[16,8,4,256]{3,2,0,1:T(4,128)S(1)} async-done(((f32[16,8,4,256]{3,2,0,1:T(4,128)}), f32[16,8,4,256]{3,2,0,1:T(4,128)S(1)}, u32[]{:S(2)}, u32[]{:S(2)}) %all-to-all-start.1) | async-done | bytes 524320 | tf_op jit(solution)/shard_map/all_to_all | solution.py:58
  103.0 0.2 reshape.271
  103.2 3.0 %scatter_custom_fusion = f32[512,256]{1,0:T(8,128)} fusion(s32[512]{0:T(512)S(1)} %bitcast.32, f32[512,256]{1,0:T(8,128)S(1)} %reshape.271, f32[]{:T(128)} %constant.100.clone.1), kind=kCustom, calls=%fused_computation.16 | custom fusion | bytes 524292 | tf_op jit(solution)/shard_map/scatter | solution.py:85
  (36 shorter events, 2.0 us)
Async XLA Ops:
  46.8 8.0 %copy-start = (s32[1,512]{1,0:T(1,128)S(1)}, s32[1,512]{1,0:T(1,128)}, u32[]{:S(2)}) copy-start(s32[1,512]{1,0:T(1,128)} %param.8) | copy-start | bytes 6148
  56.5 9.2 %all-to-all-start.2 = ((f32[4,1,256]{2,1,0:T(1,128)}), f32[4,1,256]{2,1,0:T(1,128)S(1)}, u32[]{:S(2)}, u32[]{:S(2)}) async-start(f32[4,1,256]{2,1,0:T(1,128)} %reshape.312), calls=%async_computation.2 | async-start | bytes 8192 | tf_op jit(solution)/shard_map/all_to_all | solution.py:66
  65.6 16.0 %all-to-all-start = ((f32[16,8,4,256]{3,1,0,2:T(8,128)}), f32[16,8,4,256]{3,1,0,2:T(8,128)S(1)}, u32[]{:S(2)}, u32[]{:S(2)}) async-start(f32[16,8,4,256]{3,1,0,2:T(8,128)} %copy.39), calls=%async_computation | async-start | bytes 1048576 | tf_op jit(solution)/shard_map/all_to_all | solution.py:59
  81.6 8.2 %all-to-all-start.3 = ((f32[8,1,128]{2,1,0:T(1,128)}), f32[8,1,128]{2,1,0:T(1,128)S(1)}, u32[]{:S(2)}, u32[]{:S(2)}) async-start(f32[8,1,128]{2,1,0:T(1,128)} %reshape.314), calls=%async_computation.3 | async-start | bytes 8192 | tf_op jit(solution)/shard_map/all_to_all | solution.py:65
  89.8 13.2 %all-to-all-start.1 = ((f32[16,8,4,256]{3,2,0,1:T(4,128)}), f32[16,8,4,256]{3,2,0,1:T(4,128)S(1)}, u32[]{:S(2)}, u32[]{:S(2)}) async-start(f32[16,8,4,256]{3,2,0,1:T(4,128)} %copy.40), calls=%async_computation.1 | async-start | bytes 1048576 | tf_op jit(solution)/shard_map/all_to_all | solution.py:58
where the time goes:
time: 107 us; the launch traced here: 106 us
  blocking collectives  42 us (39%)
  waiting for transfers between devices  20.1 us (19%)
  local copies, waits for them, and re-layouts  17.5 us (16%)
  starting transfers between devices  14.1 us (13%)
  matrix products  5.34 us (5%)
  other arithmetic  3.86 us (4%)
  between operations  3.41 us (3%)
    unnamed x1, blocking collectives  42 us
    all_to_all x1, waiting for transfers between devices, shards(): lax.all_to_all(outgoing[0], 'gz', split_axis=2, concat_axis=2, tiled=True)  10.3 us
    dot_general x2, matrix products, accumulate(): jnp.dot(hits.astype(jnp.float32), values, precision=lax.Precision.HIGHEST...  5.34 us
    all_to_all x1, waiting for transfers between devices, shards(): lax.all_to_all(outgoing[1], 'gz', split_axis=2, concat_axis=2, tiled=True)  4.02 us
    all_to_all x1, starting transfers between devices, shards(): lax.all_to_all(outgoing[1], 'gz', split_axis=2, concat_axis=2, tiled=True)  3.6 us
    all_to_all x1, starting transfers between devices, shards(): lax.all_to_all(lax.all_to_all(outgoing[1], 'gz', split_axis=2, concat_axi...  3.56 us
    all_to_all x1, starting transfers between devices, shards(): lax.all_to_all(lax.all_to_all(outgoing[0], 'gz', split_axis=2, concat_axi...  3.49 us
    all_to_all x1, starting transfers between devices, shards(): lax.all_to_all(outgoing[0], 'gz', split_axis=2, concat_axis=2, tiled=True)  3.47 us
  transfers between devices with their start and end apart: 4, of which 4 were waited for; matrix products, arithmetic and copies ran while one was open for 12% of the time, Pallas kernels for 0%

commit v1 on v0

--- a/solution.py
+++ b/solution.py
@@ -2,6 +2,15 @@
 import jax.numpy as jnp
 from jax import lax
 from jax.sharding import PartitionSpec as P
+
+
+def form_samples_all(view, peer_axis):
+    vec_out = lax.axis_size(peer_axis)
+    part_now = jnp.split(view, vec_out, 1)
+    res = jnp.stack(part_now, axis=0)
+    high = lax.all_to_all(res, axis_name=peer_axis, split_axis=0, concat_axis=0)
+    moved = jnp.concatenate(high, axis=1)
+    return moved
 
 
 def shards(measures, group_index, distinct_keys, group_counts):
@@ -62,12 +71,8 @@
             concat_axis=1,
             tiled=True,
         ),
-        lax.all_to_all(
-            lax.all_to_all(outgoing[1], "gz", split_axis=2, concat_axis=2, tiled=True),
-            ("gx", "gy"),
-            split_axis=1,
-            concat_axis=1,
-            tiled=True,
+        form_samples_all(
+            lax.all_to_all(outgoing[1], "gz", split_axis=2, concat_axis=2, tiled=True), ("gx", "gy")
         ),
     )
     got_sums, got_fields = arrived

time: 107 us -> 107 us (level)
    unnamed x9 -> x16, local copies, waits for them, and re-layouts: 2.18 us -> 2.24 us
where the time goes in v1:
time: 107 us; the launch traced here: 106 us
  blocking collectives  41.9 us (39%)
  waiting for transfers between devices  19.9 us (19%)
  local copies, waits for them, and re-layouts  17.5 us (16%)
  starting transfers between devices  14.1 us (13%)
  matrix products  5.34 us (5%)
  other arithmetic  3.85 us (4%)
  between operations  3.45 us (3%)
    unnamed x1, blocking collectives  41.9 us
    all_to_all x1, waiting for transfers between devices, shards(): lax.all_to_all(outgoing[0], 'gz', split_axis=2, concat_axis=2, tiled=True)  10.4 us
    dot_general x2, matrix products, accumulate(): jnp.dot(hits.astype(jnp.float32), values, precision=lax.Precision.HIGHEST...  5.34 us
    all_to_all x1, waiting for transfers between devices, shards(): lax.all_to_all(outgoing[1], 'gz', split_axis=2, concat_axis=2, tiled=True)  3.74 us
    all_to_all x1, starting transfers between devices, shards(): lax.all_to_all(outgoing[1], 'gz', split_axis=2, concat_axis=2, tiled=True)  3.59 us
    all_to_all x1, starting transfers between devices, form_samples_all(): high = lax.all_to_all(res, axis_name=peer_axis, split_axis=0, concat_axis=0)  3.55 us
    all_to_all x1, starting transfers between devices, shards(): lax.all_to_all(lax.all_to_all(outgoing[0], 'gz', split_axis=2, concat_axi...  3.49 us
    all_to_all x1, starting transfers between devices, shards(): lax.all_to_all(outgoing[0], 'gz', split_axis=2, concat_axis=2, tiled=True)  3.47 us
  transfers between devices with their start and end apart: 4, of which 4 were waited for; matrix products, arithmetic and copies ran while one was open for 12% of the time, Pallas kernels for 0%

profile of v1, /device:TPU:0, one launch (start us, length us, event | category | flops | bytes accessed | tf_op | source)
XLA Modules:
  0.0 106.2 jit_solution(10687705699491854767)
XLA Ops:
  1.4 41.9 %all-reduce = s32[32]{0:T(128)S(1)} all-reduce(s32[32]{0:T(128)S(1)} %dynamic-update-slice), channel_id=1, replica_groups=mesh['gx'=4,'gy'=2,'gz'=4] {'gx','gy','gz'}, use_global_device_ids=true, to_apply=%add | all-reduce | flops 32 | bytes 256
  43.6 0.6 fusion.20
  44.3 0.6 dynamic_slice.25
  46.8 7.4 %while.16 = (s32[]{:T(128)}, f32[512,256]{1,0:T(8,128)S(1)}, s32[512]{0:T(512)S(1)}, s32[2048]{0:T(1024)}, f32[2048,256]{1,0:T(8,128)}, /*index=5*/s32[]{:T(128)}, s32[]{:T(128)}, s32[]{:T(128)}, s32[]{:T(128)}) while((s32[]{:T(128)}, f32[512,256]{1,0:T(8,128)S(1)}, s32[512]{0:T(512)S(1)}, s32[2048]{0:T(1024)}, ...), condition=%wide.region_3.4_spmd.clone, body=%wide.region_1.3_spmd.clone.sunk | while | flops 1612972544 | bytes 2121894 | solution.py:48
  46.8 0.7 dynamic_slice.55
  47.5 2.7 %fusion.25 = f32[512,256]{1,0:T(8,128)S(1)} fusion(f32[2048,256]{1,0:T(8,128)} %get-tuple-element.211, s32[]{:T(128)S(6)} %select_n.107, s32[1024]{0:T(1024)S(1)} %dynamic_slice.55, f32[512,256]{1,0:T(8,128)S(1)} %get-tuple-element.199, pred[]{:T(512)S(6)} %compare.20), kind=kOutput, calls=%fused_computation.8.clone.1 | convolution fusion | flops 1611399168 | bytes 2101253 | tf_op jit(solution)/shard_map/while/body/eval_jaxpr/dot_general | solution.py:39
  50.2 0.3 fusion.26
  50.5 0.7 dynamic_slice.55
  51.2 2.7 %fusion.25 = f32[512,256]{1,0:T(8,128)S(1)} fusion(f32[2048,256]{1,0:T(8,128)} %get-tuple-element.211, s32[]{:T(128)S(6)} %select_n.107, s32[1024]{0:T(1024)S(1)} %dynamic_slice.55, f32[512,256]{1,0:T(8,128)S(1)} %get-tuple-element.199, pred[]{:T(512)S(6)} %compare.20), kind=kOutput, calls=%fused_computation.8.clone.1 | convolution fusion | flops 1611399168 | bytes 2101253 | tf_op jit(solution)/shard_map/while/body/eval_jaxpr/dot_general | solution.py:39
  53.9 0.3 fusion.26
  54.2 0.5 broadcast.199
  54.7 0.7 reduce.5
  55.7 0.7 reshape.312
  56.4 3.6 %all-to-all-start.2 = ((f32[4,1,256]{2,1,0:T(1,128)}), f32[4,1,256]{2,1,0:T(1,128)S(1)}, u32[]{:S(2)}, u32[]{:S(2)}) async-start(f32[4,1,256]{2,1,0:T(1,128)} %reshape.312), calls=%async_computation.2 | async-start | bytes 8192 | tf_op jit(solution)/shard_map/all_to_all | solution.py:75
  60.5 0.3 copy.59
  60.8 1.1 %copy.60 = f32[16,8,4,256]{3,1,0,2:T(8,128)} copy(f32[16,8,4,256]{3,0,2,1:T(8,128)S(1)} %bitcast.40) | data formatting | bytes 1048576 | tf_op jit(solution)/shard_map/reshape | solution.py:63
  61.9 3.7 %all-to-all-done.2 = f32[4,1,256]{2,1,0:T(1,128)S(1)} async-done(((f32[4,1,256]{2,1,0:T(1,128)}), f32[4,1,256]{2,1,0:T(1,128)S(1)}, u32[]{:S(2)}, u32[]{:S(2)}) %all-to-all-start.2) | async-done | bytes 4128 | tf_op jit(solution)/shard_map/all_to_all | solution.py:75
  65.6 3.5 %all-to-all-start = ((f32[16,8,4,256]{3,1,0,2:T(8,128)}), f32[16,8,4,256]{3,1,0,2:T(8,128)S(1)}, u32[]{:S(2)}, u32[]{:S(2)}) async-start(f32[16,8,4,256]{3,1,0,2:T(8,128)} %copy.60), calls=%async_computation | async-start | bytes 1048576 | tf_op jit(solution)/shard_map/all_to_all | solution.py:68
  69.1 0.5 broadcast.200
  69.6 0.7 reduce.6
  70.5 0.7 reshape.314
  71.2 10.4 %all-to-all-done = f32[16,8,4,256]{3,1,0,2:T(8,128)S(1)} async-done(((f32[16,8,4,256]{3,1,0,2:T(8,128)}), f32[16,8,4,256]{3,1,0,2:T(8,128)S(1)}, u32[]{:S(2)}, u32[]{:S(2)}) %all-to-all-start) | async-done | bytes 524320 | tf_op jit(solution)/shard_map/all_to_all | solution.py:68
  81.6 3.6 %all-to-all-start.3 = ((f32[8,1,128]{2,1,0:T(1,128)}), f32[8,1,128]{2,1,0:T(1,128)S(1)}, u32[]{:S(2)}, u32[]{:S(2)}) async-start(f32[8,1,128]{2,1,0:T(1,128)} %reshape.314), calls=%async_computation.3 | async-start | bytes 8192 | tf_op jit(solution)/shard_map/all_to_all | solution.py:11
  85.5 1.1 %copy.61 = f32[16,8,4,256]{3,2,0,1:T(4,128)} copy(f32[16,8,4,256]{3,1,0,2:T(8,128)S(1)} %all-to-all-done) | data formatting | bytes 1048576 | tf_op jit(solution)/shard_map/all_to_all | solution.py:68
  86.6 3.2 %all-to-all-done.3 = f32[8,1,128]{2,1,0:T(1,128)S(1)} async-done(((f32[8,1,128]{2,1,0:T(1,128)}), f32[8,1,128]{2,1,0:T(1,128)S(1)}, u32[]{:S(2)}, u32[]{:S(2)}) %all-to-all-start.3) | async-done | bytes 4128 | tf_op jit(solution)/shard_map/all_to_all | solution.py:11
  89.8 3.5 %all-to-all-start.1 = ((f32[16,8,4,256]{3,2,0,1:T(4,128)}), f32[16,8,4,256]{3,2,0,1:T(4,128)S(1)}, u32[]{:S(2)}, u32[]{:S(2)}) async-start(f32[16,8,4,256]{3,2,0,1:T(4,128)} %copy.61), calls=%async_computation.1 | async-start | bytes 1048576 | tf_op jit(solution)/shard_map/all_to_all | solution.py:67
  93.4 0.7 reduce.7
  94.4 3.0 %scatter_custom_fusion.1 = s32[512]{0:T(512)} fusion(s32[512]{0:T(512)S(1)} %bitcast.46, s32[512]{0:T(512)S(1)} %bitcast.50, s32[]{:T(128)} %constant.107.clone.1), kind=kCustom, calls=%fused_computation.48 | custom fusion | bytes 2052 | tf_op jit(solution)/shard_map/scatter | solution.py:95
  97.4 3.0 %scatter_custom_fusion.2 = s32[512]{0:T(512)} fusion(s32[512]{0:T(512)S(1)} %bitcast.47, s32[512]{0:T(512)S(1)} %bitcast.49, s32[]{:T(128)} %constant.111.clone.1), kind=kCustom, calls=%fused_computation.46 | custom fusion | bytes 2052 | tf_op jit(solution)/shard_map/scatter | solution.py:100
  100.4 2.5 %all-to-all-done.1 = f32[16,8,4,256]{3,2,0,1:T(4,128)S(1)} async-done(((f32[16,8,4,256]{3,2,0,1:T(4,128)}), f32[16,8,4,256]{3,2,0,1:T(4,128)S(1)}, u32[]{:S(2)}, u32[]{:S(2)}) %all-to-all-start.1) | async-done | bytes 524320 | tf_op jit(solution)/shard_map/all_to_all | solution.py:67
  103.0 0.2 reshape.271
  103.2 3.0 %scatter_custom_fusion = f32[512,256]{1,0:T(8,128)} fusion(s32[512]{0:T(512)S(1)} %bitcast.48, f32[512,256]{1,0:T(8,128)S(1)} %reshape.271, f32[]{:T(128)} %constant.100.clone.1), kind=kCustom, calls=%fused_computation.16 | custom fusion | bytes 524292 | tf_op jit(solution)/shard_map/scatter | solution.py:90
  (45 shorter events, 2.1 us)
Async XLA Ops:
  46.8 7.9 %copy-start = (s32[1,512]{1,0:T(1,128)S(1)}, s32[1,512]{1,0:T(1,128)}, u32[]{:S(2)}) copy-start(s32[1,512]{1,0:T(1,128)} %param.8) | copy-start | bytes 6148
  56.4 9.2 %all-to-all-start.2 = ((f32[4,1,256]{2,1,0:T(1,128)}), f32[4,1,256]{2,1,0:T(1,128)S(1)}, u32[]{:S(2)}, u32[]{:S(2)}) async-start(f32[4,1,256]{2,1,0:T(1,128)} %reshape.312), calls=%async_computation.2 | async-start | bytes 8192 | tf_op jit(solution)/shard_map/all_to_all | solution.py:75
  65.6 16.0 %all-to-all-start = ((f32[16,8,4,256]{3,1,0,2:T(8,128)}), f32[16,8,4,256]{3,1,0,2:T(8,128)S(1)}, u32[]{:S(2)}, u32[]{:S(2)}) async-start(f32[16,8,4,256]{3,1,0,2:T(8,128)} %copy.60), calls=%async_computation | async-start | bytes 1048576 | tf_op jit(solution)/shard_map/all_to_all | solution.py:68
  81.6 8.2 %all-to-all-start.3 = ((f32[8,1,128]{2,1,0:T(1,128)}), f32[8,1,128]{2,1,0:T(1,128)S(1)}, u32[]{:S(2)}, u32[]{:S(2)}) async-start(f32[8,1,128]{2,1,0:T(1,128)} %reshape.314), calls=%async_computation.3 | async-start | bytes 8192 | tf_op jit(solution)/shard_map/all_to_all | solution.py:11
  89.8 13.2 %all-to-all-start.1 = ((f32[16,8,4,256]{3,2,0,1:T(4,128)}), f32[16,8,4,256]{3,2,0,1:T(4,128)S(1)}, u32[]{:S(2)}, u32[]{:S(2)}) async-start(f32[16,8,4,256]{3,2,0,1:T(4,128)} %copy.61), calls=%async_computation.1 | async-start | bytes 1048576 | tf_op jit(solution)/shard_map/all_to_all | solution.py:67
